TPU v7x, 16 devices: a whole 2x2x2 slice. The times are simulated.
16 devices in a mesh: dp: 2 (over z), tp: 8 (over y, x, core).
Axes of the slice: x: 2, y: 2, z: 2, core: 2. Of those that a mesh axis runs over, the one named last changes fastest.
Arguments:
- x_in: bfloat16 [16, 512, 6144], P('dp', 'tp'), parts along dimension 0
- ln_gamma: float32 [6144], replicated
- ln_beta: float32 [6144], replicated
- w_q: bfloat16 [6144, 6144], P(None, 'tp')
- b_q: float32 [6144], P('tp')
- w_kv: bfloat16 [6144, 256], replicated
- b_kv: float32 [256], replicated
- w_o: bfloat16 [6144, 6144], P('tp')
- b_o: float32 [6144], replicated
- grad_y: bfloat16 [16, 512, 6144], P('dp', 'tp'), parts along dimension 0
Outputs:
- output 1: bfloat16 [16, 512, 6144], P('dp', 'tp'), parts along dimension 0
- output 2: bfloat16 [16, 512, 6144], P('dp', 'tp'), parts along dimension 0
- output 3: float32 [12288], P('dp'), parts along dimension 0
- output 4: float32 [12288], P('dp'), parts along dimension 0
- output 5: float32 [12288, 6144], P('dp', 'tp'), parts along dimension 0
- output 6: float32 [12288], P(('dp', 'tp')), parts along dimension 0
- output 7: float32 [12288, 256], P('dp'), parts along dimension 0
- output 8: float32 [512], P('dp'), parts along dimension 0
- output 9: float32 [12288, 6144], P(('dp', 'tp')), parts along dimension 0
- output 10: float32 [12288], P('dp'), parts along dimension 0
There are 2 independent parts. A program takes and returns all parts, laid end to end along the dimension named above; an argument that names none is the same for every part.
All inputs are finite; a program needn't handle non-finite values.
Results may differ from a plain program's by a relative error of at most 0.0147521.
Values are sent between devices in bfloat16 or wider.
A program may use at most 1 GiB of HBM per device.

v0:
```python
import jax
import jax.numpy as jnp
from jax import lax
from jax.sharding import PartitionSpec as P

LN_EPS = 1e-5


def norm_forward(x_loc, ln_gamma, ln_beta):
    x_wide = x_loc.astype(jnp.float32)
    centred = x_wide - jnp.mean(x_wide, axis=-1, keepdims=True)
    inv_std = lax.rsqrt(jnp.mean(centred * centred, axis=-1, keepdims=True) + LN_EPS)
    x_hat = centred * inv_std
    return x_hat, inv_std, (x_hat * ln_gamma + ln_beta).astype(jnp.bfloat16)


def norm_backward(grad_h, x_hat, inv_std, ln_gamma):
    grad_hat = grad_h * ln_gamma
    grad_in = inv_std * (grad_hat - jnp.mean(grad_hat, axis=-1, keepdims=True) - x_hat * jnp.mean(grad_hat * x_hat, axis=-1, keepdims=True))
    return grad_in, jnp.sum(grad_h * x_hat, axis=(0, 1)), jnp.sum(grad_h, axis=(0, 1))


def attn_forward(q_heads, key_rows, value_rows, causal):
    scores = jnp.einsum("bqhc,bkc->bhqk", q_heads, key_rows, preferred_element_type=jnp.float32) * q_heads.shape[-1] ** -0.5
    attn_prob = jax.nn.softmax(jnp.where(causal, scores, -1e30), axis=-1)
    prob_lo = attn_prob.astype(jnp.bfloat16)
    attended = jnp.einsum("bhqk,bkc->bqhc", prob_lo, value_rows, preferred_element_type=jnp.float32).astype(jnp.bfloat16)
    return attn_prob, prob_lo, attended


def attn_backward(grad_att, q_heads, key_rows, value_rows, attn_prob, prob_lo):
    grad_prob = jnp.einsum("bqhc,bkc->bhqk", grad_att, value_rows, preferred_element_type=jnp.float32).astype(jnp.bfloat16)
    row_dot = jnp.sum(attn_prob * grad_prob, axis=-1, keepdims=True)
    grad_score = (attn_prob * (grad_prob - row_dot) * q_heads.shape[-1] ** -0.5).astype(jnp.bfloat16)
    grad_q = jnp.einsum("bhqk,bkc->bqhc", grad_score, key_rows, preferred_element_type=jnp.float32).astype(jnp.bfloat16)
    grad_k = jnp.einsum("bhqk,bqhc->bkc", grad_score, q_heads, preferred_element_type=jnp.float32)
    grad_v = jnp.einsum("bhqk,bqhc->bkc", prob_lo, grad_att, preferred_element_type=jnp.float32)
    return grad_q, jnp.concatenate([grad_k, grad_v], axis=-1)


def solution(mesh):
    def device_block(x_loc, ln_gamma, ln_beta, w_q, b_q, w_kv, b_kv, w_o, b_o, dy_loc):
        head_dim = w_kv.shape[1] // 2
        local_heads = w_q.shape[1] // head_dim
        x_hat, inv_std, normed = norm_forward(x_loc, ln_gamma, ln_beta)
        normed_full = lax.all_gather(normed, "tp", axis=1, tiled=True)
        batch_size = normed_full.shape[0]
        seq_len = normed_full.shape[1]
        queries = (jnp.einsum("bsd,de->bse", normed_full, w_q, preferred_element_type=jnp.float32) + b_q).astype(jnp.bfloat16)
        q_heads = queries.reshape(batch_size, seq_len, local_heads, head_dim)
        key_val = (jnp.einsum("bsd,dc->bsc", normed_full, w_kv, preferred_element_type=jnp.float32) + b_kv).astype(jnp.bfloat16)
        key_rows = key_val[:, :, :head_dim]
        value_rows = key_val[:, :, head_dim:]
        positions = jnp.arange(seq_len)
        causal = positions[:, None] >= positions[None, :]
        attn_prob, prob_lo, attended = attn_forward(q_heads, key_rows, value_rows, causal)
        merged = attended.reshape(queries.shape)
        out_part = jnp.einsum("bse,ed->bsd", merged, w_o, preferred_element_type=jnp.float32).astype(jnp.bfloat16)
        out_loc = lax.psum_scatter(out_part, "tp", scatter_dimension=1, tiled=True)
        y_loc = (x_loc.astype(jnp.float32) + out_loc.astype(jnp.float32) + b_o).astype(jnp.bfloat16)

        grad_bo = lax.psum(jnp.sum(dy_loc, axis=(0, 1), dtype=jnp.float32), "tp")
        dy_full = lax.all_gather(dy_loc, "tp", axis=1, tiled=True)
        grad_wo = jnp.einsum("bse,bsd->ed", merged, dy_full, preferred_element_type=jnp.float32)
        grad_att = jnp.einsum("bsd,ed->bse", dy_full, w_o, preferred_element_type=jnp.float32).astype(jnp.bfloat16)
        grad_q, kv_wide = attn_backward(grad_att.reshape(q_heads.shape), q_heads, key_rows, value_rows, attn_prob, prob_lo)
        grad_q = grad_q.reshape(queries.shape)
        grad_kv = kv_wide.astype(jnp.bfloat16)
        grad_wq = jnp.einsum("bsd,bse->de", normed_full, grad_q, preferred_element_type=jnp.float32)
        grad_bq = jnp.sum(grad_q, axis=(0, 1), dtype=jnp.float32)
        grad_wkv, grad_bkv = lax.psum((jnp.einsum("bsd,bsc->dc", normed_full, grad_kv, preferred_element_type=jnp.float32), jnp.sum(grad_kv, axis=(0, 1), dtype=jnp.float32)), "tp")
        grad_h_part = (jnp.einsum("bse,de->bsd", grad_q, w_q, preferred_element_type=jnp.float32) + jnp.einsum("bsc,dc->bsd", grad_kv, w_kv, preferred_element_type=jnp.float32)).astype(jnp.bfloat16)
        grad_h = lax.psum_scatter(grad_h_part, "tp", scatter_dimension=1, tiled=True).astype(jnp.float32)
        grad_in, gamma_part, beta_part = norm_backward(grad_h, x_hat, inv_std, ln_gamma)
        grad_gamma, grad_beta = lax.psum((gamma_part, beta_part), "tp")
        grad_x = (dy_loc.astype(jnp.float32) + grad_in).astype(jnp.bfloat16)
        return (y_loc, grad_x, grad_gamma, grad_beta, grad_wq, grad_bq, grad_wkv, grad_bkv, grad_wo, grad_bo)

    return jax.shard_map(
        device_block,
        mesh=mesh,
        in_specs=(P("dp", "tp", None), P(None), P(None), P(None, "tp"), P("tp"), P(None, None), P(None), P("tp", None), P(None), P("dp", "tp", None)),
        out_specs=(P("dp", "tp", None), P("dp", "tp", None), P("dp"), P("dp"), P("dp", "tp"), P(("dp", "tp")), P("dp", None), P("dp"), P(("dp", "tp"), None), P("dp")),
        check_vma=False,
    )
```

profile of v0, /device:TPU:0, one launch (start us, length us, event | category | flops | bytes accessed | tf_op | source)
XLA Modules:
  0.0 1552.1 jit_solution(16253700258653315856)
XLA Ops:
  7.2 0.0 all-gather.3.cloned.1.call-start
  7.3 3.8 convert_reduce_fusion.1
  11.1 4.7 fusion.23
  15.9 0.6 copy-done.11
  16.5 6.3 fusion.20
  22.8 0.0 all-gather.5.cloned.1.call-start
  22.9 0.7 all-gather.5.cloned.1.call-update
  23.6 0.6 reduce-scatter.5.cloned.1.call-start
  24.2 0.8 iota_compare_fusion
  24.9 229.1 %all-gather.3.cloned.1.call-done = bf16[8,512,6144]{2,1,0:T(8,128)(2,1)} async-done(((bf16[8,64,6144]{2,1,0:T(8,128)(2,1)}), bf16[8,512,6144]{2,1,0:T(8,128)(2,1)}) %all-gather.3.cloned.1.call-update) | async-done | bytes 50331664 | tf_op jit(solution)/shard_map/all_gather | solution.py:46
  254.1 46.8 %add_convert_fusion.1 = bf16[8,512,768]{2,1,0:T(8,128)(2,1)} fusion(f32[768]{0:T(1024)S(1)} %copy-done.17, bf16[8,512,6144]{2,1,0:T(8,128)(2,1)} %all-gather.3.cloned.1.call-done, bf16[6144,768]{1,0:T(8,128)(2,1)} %param.13), kind=kOutput, calls=%fused_computation.50 | convolution fusion | flops 38660997120 | bytes 66063360 | tf_op jit(solution)/shard_map/bsd,de->bse/dot_general | solution.py:49
  300.9 8.6 copy.35
  309.5 174.7 %all-gather.5.cloned.1.call-done = bf16[8,512,6144]{2,1,0:T(8,128)(2,1)} async-done(((bf16[8,64,6144]{2,1,0:T(8,128)(2,1)}), bf16[8,512,6144]{2,1,0:T(8,128)(2,1)}) %all-gather.5.cloned.1.call-update) | async-done | bytes 50331664 | tf_op jit(solution)/shard_map/all_gather | solution.py:63
  484.2 47.1 %fusion.44 = bf16[8,512,768]{2,1,0:T(8,128)(2,1)} fusion(bf16[8,512,6144]{2,1,0:T(8,128)(2,1)} %all-gather.5.cloned.1.call-done, bf16[768,6144]{1,0:T(8,128)(2,1)} %param.17), kind=kOutput, calls=%fused_computation.64 | convolution fusion | flops 38657851392 | bytes 66060288 | tf_op jit(solution)/shard_map/bsd,ed->bse/dot_general | solution.py:65
  531.3 8.6 copy.40
  540.0 22.4 %add_convert_fusion.2 = bf16[8,512,256]{2,1,0:T(8,128)(2,1)} fusion(f32[256]{0:T(256)S(1)} %copy-done.18, bf16[8,512,6144]{2,1,0:T(8,128)(2,1)} %all-gather.3.cloned.1.call-done, bf16[6144,256]{1,0:T(8,128)(2,1)S(1)} %copy-done), kind=kOutput, calls=%fused_computation.62 | convolution fusion | flops 12886999040 | bytes 55575552 | tf_op jit(solution)/shard_map/bsd,dc->bsc/dot_general | solution.py:51
  562.4 14.0 convolution_convert_fusion.1
  576.4 26.5 %fusion.67 = (f32[8,6,512]{2,1,0:T(8,128)S(1)}, f32[8,6,512,512]{2,3,1,0:T(8,128)}) fusion(pred[512,512]{0,1:T(8,128)(4,1)S(1)} %copy-done.6, bf16[8,512,6,128]{1,3,2,0:T(8,128)(2,1)} %bitcast.134, bf16[8,512,256]{2,1,0:T(8,128)(2,1)} %add_convert_fusion.2), kind=kOutput, calls=%fused_computation.89 | convolution fusion | flops 3271557632 | bytes 58032128 | tf_op jit(solution)/shard_map/sub | solution.py:25
  603.0 50.6 %bitcast_convert_fusion.1 = bf16[8,512,128]{1,2,0:T(8,128)(2,1)} fusion(bf16[8,512,6,128]{1,3,2,0:T(8,128)(2,1)} %bitcast.135, bf16[8,512,512,6]{2,1,3,0:T(8,128)(2,1)} %convolution_convert_fusion.1, f32[8,6,512,512]{2,3,1,0:T(8,128)} %get-tuple-element.22, f32[8,6,512]{2,1,0:T(8,128)S(1)} %get-tuple-element.21), kind=kOutput, calls=%fused_computation.72 | convolution fusion | flops 3335021056 | bytes 82935808 | tf_op jit(solution)/shard_map/bhqk,bqhc->bkc/dot_general | solution.py:36
  653.6 51.3 %convert_reduce_fusion.3 = (f32[6,128]{1,0:T(8,128)}, bf16[8,128,6,512]{3,1,2,0:T(8,128)(2,1)}) fusion(bf16[8,512,512,6]{2,1,3,0:T(8,128)(2,1)} %convolution_convert_fusion.1, f32[8,6,512,512]{2,3,1,0:T(8,128)} %get-tuple-element.22, f32[8,6,512]{2,1,0:T(8,128)S(1)} %get-tuple-element.21, bf16[8,512,256]{2,1,0:T(8,128)(2,1)} %add_convert_fusion.2), kind=kOutput, calls=%fused_computation.45 | convolution fusion | flops 3343933184 | bytes 158600192 | tf_op jit(solution)/shard_map/bhqk,bkc->bqhc/dot_general | solution.py:35
  704.9 21.7 %bitcast_convert_fusion = bf16[8,512,128]{1,2,0:T(8,128)(2,1)} fusion(bf16[8,512,6,128]{1,3,2,0:T(8,128)(2,1)} %bitcast.133, f32[8,6,512,512]{2,3,1,0:T(8,128)} %get-tuple-element.22, f32[8,6,512]{2,1,0:T(8,128)S(1)} %get-tuple-element.21), kind=kOutput, calls=%fused_computation.71 | convolution fusion | flops 3246915584 | bytes 57769984 | tf_op jit(solution)/shard_map/bhqk,bqhc->bkc/dot_general | solution.py:37
  726.6 36.1 %fusion.50 = f32[8,512,6144]{2,1,0:T(8,128)} fusion(bf16[6144,256]{1,0:T(8,128)(2,1)S(1)} %copy-done, bf16[8,512,128]{1,2,0:T(8,128)(2,1)} %bitcast_convert_fusion, bf16[8,512,128]{1,2,0:T(8,128)(2,1)} %bitcast_convert_fusion.1), kind=kOutput, calls=%fused_computation.66 | convolution fusion | flops 12889096192 | bytes 105906176 | tf_op jit(solution)/shard_map/bsc,dc->bsd/dot_general | solution.py:72
  762.6 63.9 %add_convert_fusion = bf16[8,512,6144]{2,1,0:T(8,128)(2,1)} fusion(f32[8,512,6144]{2,1,0:T(8,128)} %fusion.50, bf16[8,512,768]{1,2,0:T(8,128)(2,1)} %bitcast.138, bf16[6144,768]{1,0:T(8,128)(2,1)} %param.13), kind=kOutput, calls=%fused_computation.2 | convolution fusion | flops 38705037312 | bytes 166723584 | tf_op jit(solution)/shard_map/bse,de->bsd/dot_general | solution.py:72
  826.5 0.0 reduce-scatter.5.cloned.1.call-update
  826.5 0.0 reduce-scatter.3.cloned.1.call-start
  826.6 1.5 copy-done.5
  828.1 20.0 %fusion.47 = bf16[8,128,6,512]{3,1,2,0:T(8,128)(2,1)} fusion(bf16[8,512,256]{2,1,0:T(8,128)(2,1)S(1)} %copy-done.5, f32[8,6,512,512]{2,3,1,0:T(8,128)} %get-tuple-element.22, f32[8,6,512]{2,1,0:T(8,128)S(1)} %get-tuple-element.21), kind=kOutput, calls=%fused_computation.65 | convolution fusion | flops 3249537024 | bytes 57802752 | tf_op jit(solution)/shard_map/bhqk,bkc->bqhc/dot_general | solution.py:27
  848.1 47.2 %convolution_convert_fusion = bf16[8,512,6144]{2,1,0:T(8,128)(2,1)} fusion(bf16[8,512,768]{1,2,0:T(8,128)(2,1)} %bitcast.136, bf16[768,6144]{1,0:T(8,128)(2,1)} %param.17), kind=kOutput, calls=%fused_computation.10 | convolution fusion | flops 38679871488 | bytes 66060288 | tf_op jit(solution)/shard_map/bse,ed->bsd/dot_general | solution.py:58
  895.4 0.0 reduce-scatter.3.cloned.1.call-update
  895.4 0.0 all-reduce.4.cloned.1.call-start
  895.4 1.1 copy-done.3
  896.6 0.3 copy-done.4
  896.9 0.9 convert_reduce_fusion.4
  897.8 23.0 %convolution_bitcast_fusion.2 = f32[6144,256]{1,0:T(8,128)} fusion(bf16[8,512,6144]{2,1,0:T(8,128)(2,1)} %all-gather.3.cloned.1.call-done, bf16[8,512,128]{1,2,0:T(8,128)(2,1)S(1)} %copy-done.4, bf16[8,512,128]{1,2,0:T(8,128)(2,1)S(1)} %copy-done.3), kind=kOutput, calls=%fused_computation.59 | convolution fusion | flops 12889096192 | bytes 58720256 | tf_op jit(solution)/shard_map/bsd,bsc->dc/dot_general | solution.py:71
  920.9 0.0 all-reduce.6.cloned.1.call-start
  920.9 47.9 %convolution_bitcast_fusion = f32[6144,768]{1,0:T(8,128)} fusion(bf16[8,512,6144]{2,1,0:T(8,128)(2,1)} %all-gather.3.cloned.1.call-done, bf16[8,512,768]{1,2,0:T(8,128)(2,1)} %bitcast.139), kind=kOutput, calls=%fused_computation.51 | convolution fusion | flops 38654705664 | bytes 75497472 | tf_op jit(solution)/shard_map/bsd,bse->de/dot_general | solution.py:69
  968.9 135.1 %reduce-scatter.5.cloned.1.call-done = bf16[8,64,6144]{2,1,0:T(8,128)(2,1)} async-done(((bf16[8,512,6144]{2,1,0:T(8,128)(2,1)}), bf16[8,64,6144]{2,1,0:T(8,128)(2,1)}) %reduce-scatter.5.cloned.1.call-update) | async-done | bytes 6291472 | tf_op jit(solution)/shard_map/reduce_scatter | solution.py:73
  1104.0 9.2 fusion.28
  1113.2 271.5 %reduce-scatter.3.cloned.1.call-done = bf16[8,64,6144]{2,1,0:T(8,128)(2,1)} async-done(((bf16[8,512,6144]{2,1,0:T(8,128)(2,1)}), bf16[8,64,6144]{2,1,0:T(8,128)(2,1)}) %reduce-scatter.3.cloned.1.call-update) | async-done | bytes 6291472 | tf_op jit(solution)/shard_map/reduce_scatter | solution.py:59
  1384.7 16.4 %convert_reduce_fusion.2 = (f32[6144]{0:T(1024)}, bf16[8,64,6144]{2,1,0:T(8,128)(2,1)}, bf16[8,64,6144]{2,1,0:T(8,128)(2,1)}) fusion(bf16[8,64,6144]{2,1,0:T(8,128)(2,1)} %param.19, f32[8,64]{1,0:T(8,128)S(1)} %get-tuple-element.25, f32[8,64]{1,0:T(8,128)S(1)} %copy-done.10, bf16[8,64,6144]{2,1,0:T(8,128)(2,1)} %param.10, f32[8,64]{1,0:T(8,128)S(1)} %get-tuple-element.26, ...), kind=kLoop, calls=%fused_computation.28 | loop fusion | flops 53471232 | bytes 37830656 | tf_op jit(solution)/shard_map/reduce_sum | solution.py:62
  1401.1 47.2 %convolution_bitcast_fusion.1 = f32[768,6144]{1,0:T(8,128)} fusion(bf16[8,512,768]{1,2,0:T(8,128)(2,1)} %bitcast.137, bf16[8,512,6144]{2,1,0:T(8,128)(2,1)} %all-gather.5.cloned.1.call-done), kind=kOutput, calls=%fused_computation.52 | convolution fusion | flops 38654705664 | bytes 75497472 | tf_op jit(solution)/shard_map/bse,bsd->ed/dot_general | solution.py:64
  1448.3 35.6 %all-reduce.4.cloned.1.call-done = f32[6144,256]{1,0:T(8,128)} async-done(((f32[6144,256]{1,0:T(8,128)}), f32[6144,256]{1,0:T(8,128)}) %all-reduce.4.cloned.1.call-update) | async-done | bytes 6291472 | tf_op jit(solution)/shard_map/psum | solution.py:71
  1483.8 51.4 %all-reduce.6.cloned.1.call-done = (f32[6144]{0:T(1024)}, f32[6144]{0:T(1024)}, f32[256]{0:T(256)}, f32[6144]{0:T(1024)}) async-done(((f32[6144]{0:T(1024)}, f32[6144]{0:T(1024)}, f32[256]{0:T(256)}, f32[6144]{0:T(1024)}), (f32[6144]{0:T(1024)}, f32[6144]{0:T(1024)}, f32[256]{0:T(256)}, f32[6144]{0:T(1024)})) %all-reduce.6.cloned.1.call-update) | async-done | bytes 74768 | tf_op jit(solution)/shard_map/psum | solution.py:75
  1535.2 1.4 copy.76
  1536.6 1.3 copy.77
  1537.9 5.9 copy.78
  1543.8 0.6 copy.79
  1544.4 0.6 copy.80
  (40 shorter events, 0.2 us)
Async XLA Ops:
  7.2 532.8 %copy-start = (bf16[6144,256]{1,0:T(8,128)(2,1)S(1)}, bf16[6144,256]{1,0:T(8,128)(2,1)}, u32[]{:S(2)}) copy-start(bf16[6144,256]{1,0:T(8,128)(2,1)} %param.15) | copy-start | bytes 9437188
  7.2 9.3 copy-start.7
  7.2 9.2 copy-start.15
  7.2 246.8 %all-gather.3.cloned.1.call-start = ((), (), s32[]{:S(2)}) async-start(), calls=%async_computation.2 | async-start | bytes 56623104 | tf_op jit(solution)/shard_map/all_gather | solution.py:46
  7.3 9.2 copy-start.2
  11.1 4.7 copy-start.9
  15.8 0.6 copy-start.11
  16.5 237.6 %copy-start.17 = (f32[768]{0:T(1024)S(1)}, f32[768]{0:T(1024)}, u32[]{:S(2)}) copy-start(f32[768]{0:T(1024)} %param.14) | copy-start | bytes 9220
  22.8 461.4 %all-gather.5.cloned.1.call-start = ((), (), s32[]{:S(2)}) async-start(), calls=%async_computation.4 | async-start | bytes 56623104 | tf_op jit(solution)/shard_map/all_gather | solution.py:63
  23.6 1080.4 %reduce-scatter.5.cloned.1.call-start = ((), (), s32[]{:S(2)}) async-start(), calls=%async_computation.5 | async-start | bytes 56623104 | tf_op jit(solution)/shard_map/reduce_scatter | solution.py:73
  531.3 8.6 copy-start.18
  562.4 14.0 copy-start.6
  826.5 1.6 copy-start.5
  826.5 558.1 %reduce-scatter.3.cloned.1.call-start = ((), (), s32[]{:S(2)}) async-start(), calls=%async_computation.3 | async-start | bytes 56623104 | tf_op jit(solution)/shard_map/reduce_scatter | solution.py:59
  895.4 1.2 copy-start.3
  895.4 1.5 copy-start.4
  895.4 588.5 %all-reduce.4.cloned.1.call-start = ((), (), s32[]{:S(2)}) async-start(), calls=%async_computation.6 | async-start | bytes 12582912 | tf_op jit(solution)/shard_map/psum | solution.py:71
  920.8 183.1 %copy-start.8 = (f32[6144]{0:T(1024)S(1)}, f32[6144]{0:T(1024)}, u32[]{:S(2)}) copy-start(f32[6144]{0:T(1024)} %param.11) | copy-start | bytes 73732
  920.9 183.1 %copy-start.10 = (f32[8,64]{1,0:T(8,128)S(1)}, f32[8,64]{1,0:T(8,128)}, u32[]{:S(2)}) copy-start(f32[8,64]{1,0:T(8,128)} %copy-done.9) | copy-start | bytes 6148
  920.9 183.1 %copy-start.12 = (f32[8,64]{1,0:T(8,128)S(1)}, f32[8,64]{1,0:T(8,128)}, u32[]{:S(2)}) copy-start(f32[8,64]{1,0:T(8,128)} %copy-done.11) | copy-start | bytes 6148
  920.9 614.4 %all-reduce.6.cloned.1.call-start = ((), (), s32[]{:S(2)}) async-start(), calls=%async_computation.7 | async-start | bytes 149504 | tf_op jit(solution)/shard_map/psum | solution.py:75
  968.9 415.8 %copy-start.13 = (f32[6144]{0:T(1024)S(1)}, f32[6144]{0:T(1024)}, u32[]{:S(2)}) copy-start(f32[6144]{0:T(1024)} %param.18) | copy-start | bytes 73732
  1401.1 143.9 %copy-start.1 = (bf16[6144,256]{1,0:T(8,128)(2,1)S(1)}, bf16[6144,256]{1,0:T(8,128)(2,1)}, u32[]{:S(2)}) copy-start(bf16[6144,256]{1,0:T(8,128)(2,1)} %param.15) | copy-start | bytes 9437188
  1535.2 8.6 copy-start.16
  1535.2 9.2 copy-start.14
Sparse Core Ops, SparseCore 0:
  22.9 231.0 all-gather.2
  255.9 228.2 all-gather.4
  826.7 277.2 reduce-scatter.4
  1107.4 277.2 reduce-scatter.2
  1387.8 95.9 all-reduce.3
  1488.3 46.8 all-reduce.5
where the time goes:
time: 1560 us; the launch traced here: 1550 us
  waiting for transfers between devices  898 us (58%)
  matrix products  566 us (36%)
  other arithmetic  42.2 us (3%)
  local copies, waits for them, and re-layouts  30.7 us (2%)
    reduce_scatter x1, waiting for transfers between devices, device_block(): out_loc = lax.psum_scatter(out_part, 'tp', scatter_dimension=1, tiled=True)  271 us
    all_gather x1, waiting for transfers between devices, device_block(): normed_full = lax.all_gather(normed, 'tp', axis=1, tiled=True)  229 us
    all_gather x1, waiting for transfers between devices, device_block(): dy_full = lax.all_gather(dy_loc, 'tp', axis=1, tiled=True)  175 us
    reduce_scatter x1, waiting for transfers between devices, device_block(): lax.psum_scatter(grad_h_part, 'tp', scatter_dimension=1, tiled=True)  135 us
    dot_general x1, matrix products, device_block(): jnp.einsum('bse,de->bsd', grad_q, w_q, preferred_element_type=jnp.float32)  63.9 us
    psum x1, waiting for transfers between devices, device_block(): grad_gamma, grad_beta = lax.psum((gamma_part, beta_part), 'tp')  51.4 us
    dot_general x1, matrix products, attn_backward(): jnp.einsum('bhqk,bkc->bqhc', grad_score, key_rows, preferred_element_type...  51.3 us
    dot_general x1, matrix products, attn_backward(): jnp.einsum('bhqk,bqhc->bkc', grad_score, q_heads, preferred_element_type=...  50.6 us
  transfers between devices with their start and end apart: 6, of which 6 were waited for; matrix products, arithmetic and copies ran while one was open for 17% of the time, Pallas kernels for 0%

commit v1 on v0

v1 whole, which is shorter than its diff:
```python
import jax
import jax.numpy as jnp
from jax import lax
from jax.sharding import PartitionSpec as P


LN_EPS = 1e-5
CHUNKS = 2


def norm_forward(x_loc, ln_gamma, ln_beta):
    x_wide = x_loc.astype(jnp.float32)
    centred = x_wide - jnp.mean(x_wide, axis=-1, keepdims=True)
    inv_std = lax.rsqrt(jnp.mean(centred * centred, axis=-1, keepdims=True) + LN_EPS)
    x_hat = centred * inv_std
    return x_hat, inv_std, (x_hat * ln_gamma + ln_beta).astype(jnp.bfloat16)


def norm_backward(grad_h, x_hat, inv_std, ln_gamma):
    grad_hat = grad_h * ln_gamma
    grad_in = inv_std * (grad_hat - jnp.mean(grad_hat, axis=-1, keepdims=True) - x_hat * jnp.mean(grad_hat * x_hat, axis=-1, keepdims=True))
    return grad_in, jnp.sum(grad_h * x_hat, axis=(0, 1)), jnp.sum(grad_h, axis=(0, 1))


def attn_forward(q_heads, key_rows, value_rows, causal):
    scores = jnp.einsum("bqhc,bkc->bhqk", q_heads, key_rows, preferred_element_type=jnp.float32) * q_heads.shape[-1] ** -0.5
    attn_prob = jax.nn.softmax(jnp.where(causal, scores, -1e30), axis=-1)
    prob_lo = attn_prob.astype(jnp.bfloat16)
    attended = jnp.einsum("bhqk,bkc->bqhc", prob_lo, value_rows, preferred_element_type=jnp.float32).astype(jnp.bfloat16)
    return attn_prob, prob_lo, attended


def attn_backward(grad_att, q_heads, key_rows, value_rows, attn_prob, prob_lo):
    grad_prob = jnp.einsum("bqhc,bkc->bhqk", grad_att, value_rows, preferred_element_type=jnp.float32).astype(jnp.bfloat16)
    row_dot = jnp.sum(attn_prob * grad_prob, axis=-1, keepdims=True)
    grad_score = (attn_prob * (grad_prob - row_dot) * q_heads.shape[-1] ** -0.5).astype(jnp.bfloat16)
    grad_q = jnp.einsum("bhqk,bkc->bqhc", grad_score, key_rows, preferred_element_type=jnp.float32).astype(jnp.bfloat16)
    grad_k = jnp.einsum("bhqk,bqhc->bkc", grad_score, q_heads, preferred_element_type=jnp.float32)
    grad_v = jnp.einsum("bhqk,bqhc->bkc", prob_lo, grad_att, preferred_element_type=jnp.float32)
    return grad_q, jnp.concatenate([grad_k, grad_v], axis=-1)


def solution(mesh):
    def device_block(x_loc, ln_gamma, ln_beta, w_q, b_q, w_kv, b_kv, w_o, b_o, dy_loc):
        head_dim = w_kv.shape[1] // 2
        local_heads = w_q.shape[1] // head_dim
        per = x_loc.shape[0] // CHUNKS
        local_len = x_loc.shape[1]
        cut = lambda a, c: a[c * per:(c + 1) * per]
        xs = [cut(x_loc, c) for c in range(CHUNKS)]
        dys = [cut(dy_loc, c) for c in range(CHUNKS)]
        norms = [norm_forward(xc, ln_gamma, ln_beta) for xc in xs]
        gather = lambda a: lax.all_gather(a, "tp", axis=1, tiled=True)
        h_full, dy_full = [], []
        for c in range(CHUNKS):
            dy_full.append(gather(dys[c]))
            h_full.append(gather(norms[c][2]))
        grad_bo_part = jnp.sum(dy_loc, axis=(0, 1), dtype=jnp.float32)

        y_parts, dh_parts, kv_parts = [], [], []
        grad_wq = grad_wo = grad_bq = 0.0
        for c in range(CHUNKS):
            hc, dyc = h_full[c], dy_full[c]
            if c:
                hc, _, _ = lax.optimization_barrier((hc, out_part, dh_part))
            seq_len = hc.shape[1]
            positions = jnp.arange(seq_len)
            causal = positions[:, None] >= positions[None, :]
            queries = (jnp.einsum("bsd,de->bse", hc, w_q, preferred_element_type=jnp.float32) + b_q).astype(jnp.bfloat16)
            if c:
                dyc, _ = lax.optimization_barrier((dyc, queries))
            q_heads = queries.reshape(per, seq_len, local_heads, head_dim)
            key_val = (jnp.einsum("bsd,dc->bsc", hc, w_kv, preferred_element_type=jnp.float32) + b_kv).astype(jnp.bfloat16)
            key_rows = key_val[:, :, :head_dim]
            value_rows = key_val[:, :, head_dim:]
            attn_prob, prob_lo, attended = attn_forward(q_heads, key_rows, value_rows, causal)
            merged = attended.reshape(queries.shape)
            out_part = jnp.einsum("bse,ed->bsd", merged, w_o, preferred_element_type=jnp.float32).astype(jnp.bfloat16)
            y_parts.append(lax.psum_scatter(out_part, "tp", scatter_dimension=1, tiled=True))
            grad_att = jnp.einsum("bsd,ed->bse", dyc, w_o, preferred_element_type=jnp.float32).astype(jnp.bfloat16)
            grad_q, kv_wide = attn_backward(grad_att.reshape(q_heads.shape), q_heads, key_rows, value_rows, attn_prob, prob_lo)
            grad_q = grad_q.reshape(queries.shape)
            kv_parts.append(kv_wide.astype(jnp.bfloat16))
            dh_part = jnp.einsum("bse,de->bsd", grad_q, w_q, preferred_element_type=jnp.float32).astype(jnp.bfloat16)
            dh_parts.append(lax.psum_scatter(dh_part, "tp", scatter_dimension=1, tiled=True))
            grad_wq += jnp.einsum("bsd,bse->de", hc, grad_q, preferred_element_type=jnp.float32)
            grad_wo += jnp.einsum("bse,bsd->ed", merged, dyc, preferred_element_type=jnp.float32)
            grad_bq += jnp.sum(grad_q, axis=(0, 1), dtype=jnp.float32)

        kv_sent = jnp.concatenate(kv_parts, axis=0)
        kv_got = lax.all_to_all(kv_sent, "tp", split_axis=1, concat_axis=1, tiled=True)
        kv_got = kv_got.reshape(kv_got.shape[0], -1, local_len, kv_got.shape[2])
        kv_at = jnp.sum(kv_got.astype(jnp.float32), axis=1).astype(jnp.bfloat16)
        pieces = [gather(kv_at[i:i + 2]) for i in range(0, kv_at.shape[0], 2)]
        grad_kv = jnp.concatenate(pieces, axis=0)
        grad_wkv = sum(jnp.einsum("bsd,bsc->dc", h_full[c], cut(grad_kv, c), preferred_element_type=jnp.float32) for c in range(CHUNKS))
        grad_bkv = jnp.sum(grad_kv, axis=(0, 1), dtype=jnp.float32)
        dh_kv = jnp.einsum("bsc,dc->bsd", kv_at, w_kv, preferred_element_type=jnp.float32)

        dxs = []
        gamma_part = beta_part = 0.0
        for c in range(CHUNKS):
            if c:
                dh_parts[c], _, _, _ = lax.optimization_barrier((dh_parts[c], dxs[-1], gamma_part, beta_part))
            x_hat, inv_std, _ = norms[c]
            grad_h = dh_parts[c].astype(jnp.float32) + cut(dh_kv, c)
            grad_in, g_part, b_part = norm_backward(grad_h, x_hat, inv_std, ln_gamma)
            gamma_part += g_part
            beta_part += b_part
            dxs.append((dys[c].astype(jnp.float32) + grad_in).astype(jnp.bfloat16))
        grad_x = jnp.concatenate(dxs, axis=0)
        y_parts[-1], grad_x, grad_wkv, grad_bkv = lax.optimization_barrier((y_parts[-1], grad_x, grad_wkv, grad_bkv))
        ys = [(xs[c].astype(jnp.float32) + y_parts[c].astype(jnp.float32) + b_o).astype(jnp.bfloat16) for c in range(CHUNKS)]
        smalls = lax.all_gather(jnp.stack([gamma_part, beta_part, grad_bo_part]), "tp", axis=0)
        grad_gamma, grad_beta, grad_bo = jnp.sum(smalls, axis=0)
        return (jnp.concatenate(ys, axis=0), grad_x, grad_gamma, grad_beta, grad_wq, grad_bq, grad_wkv, grad_bkv, grad_wo, grad_bo)

    return jax.shard_map(
        device_block,
        mesh=mesh,
        in_specs=(P("dp", "tp", None), P(None), P(None), P(None, "tp"), P("tp"), P(None, None), P(None), P("tp", None), P(None), P("dp", "tp", None)),
        out_specs=(P("dp", "tp", None), P("dp", "tp", None), P("dp"), P("dp"), P("dp", "tp"), P(("dp", "tp")), P("dp", None), P("dp"), P(("dp", "tp"), None), P("dp")),
        check_vma=False,
    )
```

time: 1560 us -> 1180 us (0.76)
  waiting for transfers between devices: 898 us -> 381 us
  blocking collectives: 0 us -> 60.2 us
  matrix products: 566 us -> 611 us
  other arithmetic: 42.2 us -> 68.6 us
    reduce_scatter x2 -> x4, waiting for transfers between devices: 407 us -> 117 us  [the longest x2 117 us: device_block(): lax.psum_scatter(out_part, 'tp', scatter_dimension=1, tiled=True)]
    all_gather x2 -> x4, waiting for transfers between devices: 404 us -> 263 us  [device_block(): gather = lambda a: lax.all_gather(a, 'tp', axis=1, tiled=True)]
    psum x2 -> x0, waiting for transfers between devices: 87 us -> none  [the longest x1 51.4 us: device_block(): grad_gamma, grad_beta = lax.psum((gamma_part, beta_part), 'tp')]
    all_gather x0 -> x5, blocking collectives: none -> 60.2 us  [the longest x4 49.5 us: device_block(): gather = lambda a: lax.all_gather(a, 'tp', axis=1, tiled=True)]
    convert_element_type x0 -> x3, other arithmetic: none -> 23 us  [the longest x2 17.2 us: device_block(): dxs.append((dys[c].astype(jnp.float32) + grad_in).astype(jnp.bfloat16))]
    dot_general x7 -> x13, matrix products: 271 us -> 285 us  [the longest x2 60.3 us: device_block(): jnp.einsum('bse,bsd->ed', merged, dyc, preferred_element_type=jnp.float32)]
    dot_general x1 -> x2, matrix products: 50.6 us -> 60.8 us  [attn_backward(): jnp.einsum('bhqk,bqhc->bkc', grad_score, q_heads, preferred_element_type=...]
    dot_general x1 -> x2, matrix products: 63.9 us -> 53.9 us  [device_block(): jnp.einsum('bse,de->bsd', grad_q, w_q, preferred_element_type=jnp.float32)]
  transfers between devices with their start and end apart: 6 -> 9, of which waited for: 6 -> 4; matrix products, arithmetic and copies ran while one was open for 17% -> 59% of each run, Pallas kernels for 0% -> 0%
where the time goes in v1:
time: 1180 us
  matrix products  611 us (52%)
  waiting for transfers between devices  381 us (32%)
  other arithmetic  68.6 us (6%)
  blocking collectives  60.2 us (5%)
  local copies, waits for them, and re-layouts  37.3 us (3%)
  between operations  14.9 us (1%)
    all_gather x4, waiting for transfers between devices, device_block(): gather = lambda a: lax.all_gather(a, 'tp', axis=1, tiled=True)  263 us
    reduce_scatter x2, waiting for transfers between devices, device_block(): lax.psum_scatter(out_part, 'tp', scatter_dimension=1, tiled=True)  117 us
    dot_general x2, matrix products, attn_backward(): jnp.einsum('bhqk,bqhc->bkc', grad_score, q_heads, preferred_element_type=...  60.8 us
    dot_general x2, matrix products, device_block(): jnp.einsum('bse,bsd->ed', merged, dyc, preferred_element_type=jnp.float32)  60.3 us
    dot_general x2, matrix products, attn_backward(): jnp.einsum('bhqk,bkc->bqhc', grad_score, key_rows, preferred_element_type...  60 us
    dot_general x2, matrix products, device_block(): jnp.einsum('bsd,bse->de', hc, grad_q, preferred_element_type=jnp.float32)  59.9 us
    dot_general x2, matrix products, device_block(): jnp.einsum('bse,ed->bsd', merged, w_o, preferred_element_type=jnp.float32)  55.5 us
    dot_general x2, matrix products, device_block(): jnp.einsum('bse,de->bsd', grad_q, w_q, preferred_element_type=jnp.float32)  53.9 us
  transfers between devices with their start and end apart: 9, of which 4 were waited for; matrix products, arithmetic and copies ran while one was open for 59% of the time, Pallas kernels for 0%

profile of v1, /device:TPU:0, one launch (start us, length us, event | category | flops | bytes accessed | tf_op | source)
XLA Modules:
  0.0 1178.9 jit_solution(11733354945381404932)
XLA Ops:
  18.8 6.3 fusion.152
  26.6 116.6 %all-gather.7.cloned.1.call-done = bf16[4,512,6144]{2,1,0:T(8,128)(2,1)} async-done(((bf16[4,64,6144]{2,1,0:T(8,128)(2,1)}), bf16[4,512,6144]{2,1,0:T(8,128)(2,1)}) %all-gather.7.cloned.1.call-update) | async-done | bytes 25165840 | tf_op jit(solution)/shard_map/all_gather | solution.py:53
  143.1 26.7 %add_convert_fusion.1 = bf16[4,512,768]{2,1,0:T(8,128)(2,1)} fusion(f32[768]{0:T(1024)S(1)} %copy-done.30, bf16[4,512,6144]{2,1,0:T(8,128)(2,1)} %all-gather.7.cloned.1.call-done, bf16[6144,768]{1,0:T(8,128)(2,1)} %param.13), kind=kOutput, calls=%fused_computation.113 | convolution fusion | flops 19330498560 | bytes 37751808 | tf_op jit(solution)/shard_map/bsd,de->bse/dot_general | solution.py:69
  174.5 92.6 %all-gather.11.cloned.1.call-done = bf16[4,512,6144]{2,1,0:T(8,128)(2,1)} async-done(((bf16[4,64,6144]{2,1,0:T(8,128)(2,1)}), bf16[4,512,6144]{2,1,0:T(8,128)(2,1)}) %all-gather.11.cloned.1.call-update) | async-done | bytes 25165840 | tf_op jit(solution)/shard_map/all_gather | solution.py:53
  267.1 26.7 %fusion.101 = bf16[4,512,768]{2,1,0:T(8,128)(2,1)} fusion(bf16[4,512,6144]{2,1,0:T(8,128)(2,1)} %all-gather.11.cloned.1.call-done, bf16[768,6144]{1,0:T(8,128)(2,1)} %param.17), kind=kOutput, calls=%fused_computation.129 | convolution fusion | flops 19328925696 | bytes 37748736 | tf_op jit(solution)/shard_map/bsd,ed->bse/dot_general | solution.py:80
  293.8 4.7 copy.80
  298.5 11.9 %add_convert_fusion.3 = bf16[4,512,256]{2,1,0:T(8,128)(2,1)S(1)} fusion(bf16[4,512,6144]{2,1,0:T(8,128)(2,1)} %all-gather.7.cloned.1.call-done, bf16[6144,256]{1,0:T(8,128)(2,1)S(1)} %copy-done, f32[256]{0:T(256)S(1)} %copy-done.32), kind=kOutput, calls=%fused_computation.133 | convolution fusion | flops 6443499520 | bytes 29361152 | tf_op jit(solution)/shard_map/bsd,dc->bsc/dot_general | solution.py:73
  310.4 6.8 convolution_convert_fusion.5
  317.2 15.4 %fusion.155 = (f32[4,6,512]{2,1,0:T(8,128)S(1)}, f32[4,6,512,512]{2,3,1,0:T(8,128)}) fusion(pred[512,512]{0,1:T(8,128)(4,1)S(1)} %iota_compare_fusion, bf16[4,512,6,128]{1,3,2,0:T(8,128)(2,1)} %bitcast.292, bf16[4,512,256]{2,1,0:T(8,128)(2,1)} %copy-done.14), kind=kOutput, calls=%fused_computation.185 | convolution fusion | flops 1635779072 | bytes 29147136 | tf_op jit(solution)/shard_map/sub | solution.py:27
  332.6 29.5 %convert_reduce_fusion.4 = (f32[6,128]{1,0:T(8,128)}, bf16[4,128,6,512]{3,1,2,0:T(8,128)(2,1)}) fusion(bf16[4,512,512,6]{2,1,3,0:T(8,128)(2,1)} %convolution_convert_fusion.5, f32[4,6,512,512]{2,3,1,0:T(8,128)} %get-tuple-element.50, f32[4,6,512]{2,1,0:T(8,128)S(1)} %get-tuple-element.49, bf16[4,512,256]{2,1,0:T(8,128)(2,1)} %copy-done.14), kind=kOutput, calls=%fused_computation.103 | convolution fusion | flops 1671966464 | bytes 79301632 | tf_op jit(solution)/shard_map/bhqk,bkc->bqhc/dot_general | solution.py:37
  362.1 27.0 %convolution_convert_fusion.2 = bf16[4,512,6144]{2,1,0:T(8,128)(2,1)} fusion(bf16[4,512,768]{1,2,0:T(8,128)(2,1)} %bitcast.302, bf16[6144,768]{1,0:T(8,128)(2,1)} %param.13), kind=kOutput, calls=%fused_computation.26 | convolution fusion | flops 19339935744 | bytes 37748736 | tf_op jit(solution)/shard_map/bse,de->bsd/dot_general | solution.py:84
  389.2 10.4 fusion.95
  401.3 28.4 %convolution_convert_fusion.3 = bf16[4,512,6144]{2,1,0:T(8,128)(2,1)} fusion(bf16[4,512,768]{1,2,0:T(8,128)(2,1)S(1)} %bitcast.304, bf16[768,6144]{1,0:T(8,128)(2,1)} %param.17), kind=kOutput, calls=%fused_computation.27 | convolution fusion | flops 19339935744 | bytes 37748736 | tf_op jit(solution)/shard_map/bse,ed->bsd/dot_general | solution.py:78
  429.7 26.6 %add_convert_fusion = bf16[4,512,768]{2,1,0:T(8,128)(2,1)} fusion(f32[768]{0:T(1024)S(1)} %copy-done.31, bf16[4,512,6144]{2,1,0:T(8,128)(2,1)} %all-gather.9.cloned.1.call-done, bf16[6144,768]{1,0:T(8,128)(2,1)} %param.13), kind=kOutput, calls=%fused_computation.108 | convolution fusion | flops 19330498560 | bytes 37751808 | tf_op jit(solution)/shard_map/bsd,de->bse/dot_general | solution.py:69
  460.9 53.8 %all-gather.13.cloned.1.call-done = bf16[4,512,6144]{2,1,0:T(8,128)(2,1)} async-done(((bf16[4,64,6144]{2,1,0:T(8,128)(2,1)}), bf16[4,512,6144]{2,1,0:T(8,128)(2,1)}) %all-gather.13.cloned.1.call-update) | async-done | bytes 25165840 | tf_op jit(solution)/shard_map/all_gather | solution.py:53
  514.7 26.9 %fusion.104 = bf16[4,512,768]{2,1,0:T(8,128)(2,1)} fusion(bf16[4,512,6144]{2,1,0:T(8,128)(2,1)} %all-gather.13.cloned.1.call-done, bf16[768,6144]{1,0:T(8,128)(2,1)} %param.17), kind=kOutput, calls=%fused_computation.130 | convolution fusion | flops 19328925696 | bytes 37748736 | tf_op jit(solution)/shard_map/bsd,ed->bse/dot_general | solution.py:80
  541.7 5.2 copy.92
  546.9 12.5 %add_convert_fusion.2 = bf16[4,512,256]{2,1,0:T(8,128)(2,1)S(1)} fusion(bf16[4,512,6144]{2,1,0:T(8,128)(2,1)} %all-gather.9.cloned.1.call-done, bf16[6144,256]{1,0:T(8,128)(2,1)S(1)} %copy-done, f32[256]{0:T(256)S(1)} %copy-done.33), kind=kOutput, calls=%fused_computation.132 | convolution fusion | flops 6443499520 | bytes 29361152 | tf_op jit(solution)/shard_map/bsd,dc->bsc/dot_general | solution.py:73
  559.5 6.6 convolution_convert_fusion.4
  566.1 15.8 %fusion.156 = (f32[4,6,512]{2,1,0:T(8,128)S(1)}, f32[4,6,512,512]{2,3,1,0:T(8,128)}) fusion(pred[512,512]{0,1:T(8,128)(4,1)S(1)} %copy-done.16, bf16[4,512,6,128]{1,3,2,0:T(8,128)(2,1)} %bitcast.294, bf16[4,512,256]{2,1,0:T(8,128)(2,1)} %copy-done.13), kind=kOutput, calls=%fused_computation.186 | convolution fusion | flops 1635779072 | bytes 29147136 | tf_op jit(solution)/shard_map/sub | solution.py:27
  581.9 30.5 %convert_reduce_fusion.3 = (f32[6,128]{1,0:T(8,128)}, bf16[4,128,6,512]{3,1,2,0:T(8,128)(2,1)}) fusion(bf16[4,512,512,6]{2,1,3,0:T(8,128)(2,1)} %convolution_convert_fusion.4, f32[4,6,512,512]{2,3,1,0:T(8,128)} %get-tuple-element.52, f32[4,6,512]{2,1,0:T(8,128)S(1)} %get-tuple-element.51, bf16[4,512,256]{2,1,0:T(8,128)(2,1)} %copy-done.13), kind=kOutput, calls=%fused_computation.102 | convolution fusion | flops 1671966464 | bytes 79301632 | tf_op jit(solution)/shard_map/bhqk,bkc->bqhc/dot_general | solution.py:37
  612.3 26.9 %convolution_convert_fusion = bf16[4,512,6144]{2,1,0:T(8,128)(2,1)} fusion(bf16[4,512,768]{1,2,0:T(8,128)(2,1)} %bitcast.306, bf16[6144,768]{1,0:T(8,128)(2,1)} %param.13), kind=kOutput, calls=%fused_computation.24 | convolution fusion | flops 19339935744 | bytes 37748736 | tf_op jit(solution)/shard_map/bse,de->bsd/dot_general | solution.py:84
  639.3 11.0 fusion.98
  652.0 27.1 %convolution_convert_fusion.1 = bf16[4,512,6144]{2,1,0:T(8,128)(2,1)} fusion(bf16[4,512,768]{1,2,0:T(8,128)(2,1)S(1)} %bitcast.308, bf16[768,6144]{1,0:T(8,128)(2,1)} %param.17), kind=kOutput, calls=%fused_computation.25 | convolution fusion | flops 19339935744 | bytes 37748736 | tf_op jit(solution)/shard_map/bse,ed->bsd/dot_general | solution.py:78
  679.2 6.9 convert_reduce_fusion
  686.1 17.8 %fusion.124 = bf16[4,512,128]{1,2,0:T(8,128)(2,1)} fusion(bf16[4,512,6,128]{1,3,2,0:T(8,128)(2,1)S(1)} %bitcast.289, f32[4,6,512,512]{2,3,1,0:T(8,128)} %get-tuple-element.50, f32[4,6,512]{2,1,0:T(8,128)S(1)} %copy-done.39), kind=kOutput, calls=%fused_computation.141 | convolution fusion | flops 1623457792 | bytes 28884992 | tf_op jit(solution)/shard_map/bhqk,bqhc->bkc/dot_general | solution.py:39
  704.0 30.4 %fusion.119 = bf16[4,512,128]{1,2,0:T(8,128)(2,1)} fusion(bf16[4,512,6,128]{1,3,2,0:T(8,128)(2,1)} %bitcast.293, bf16[4,512,512,6]{2,1,3,0:T(8,128)(2,1)} %convolution_convert_fusion.5, f32[4,6,512,512]{2,3,1,0:T(8,128)} %get-tuple-element.50, f32[4,6,512]{2,1,0:T(8,128)S(1)} %copy-done.39), kind=kOutput, calls=%fused_computation.138 | convolution fusion | flops 1667510784 | bytes 41467904 | tf_op jit(solution)/shard_map/bhqk,bqhc->bkc/dot_general | solution.py:38
  734.4 30.4 %fusion.120 = bf16[4,512,128]{1,2,0:T(8,128)(2,1)} fusion(bf16[4,512,6,128]{1,3,2,0:T(8,128)(2,1)} %bitcast.295, bf16[4,512,512,6]{2,1,3,0:T(8,128)(2,1)} %convolution_convert_fusion.4, f32[4,6,512,512]{2,3,1,0:T(8,128)} %get-tuple-element.52, f32[4,6,512]{2,1,0:T(8,128)S(1)} %get-tuple-element.51), kind=kOutput, calls=%fused_computation.139 | convolution fusion | flops 1667510784 | bytes 41467904 | tf_op jit(solution)/shard_map/bhqk,bqhc->bkc/dot_general | solution.py:38
  764.8 11.9 %fusion.121 = bf16[4,512,128]{1,2,0:T(8,128)(2,1)S(1)} fusion(bf16[4,512,6,128]{1,3,2,0:T(8,128)(2,1)} %bitcast.290, f32[4,6,512,512]{2,3,1,0:T(8,128)} %get-tuple-element.52, f32[4,6,512]{2,1,0:T(8,128)S(1)} %get-tuple-element.51), kind=kOutput, calls=%fused_computation.140 | convolution fusion | flops 1623457792 | bytes 28884992 | tf_op jit(solution)/shard_map/bhqk,bqhc->bkc/dot_general | solution.py:39
  782.7 4.8 all-to-all-start
  787.5 26.6 %fusion.157 = f32[6144,768,1]{1,0,2:T(8,128)} fusion(bf16[4,512,6144]{2,1,0:T(8,128)(2,1)} %all-gather.7.cloned.1.call-done, bf16[4,512,768]{1,2,0:T(8,128)(2,1)} %bitcast.303), kind=kOutput, calls=%fused_computation.187 | convolution fusion | flops 19327352832 | bytes 47185920 | tf_op jit(solution)/shard_map/bsd,bse->de/dot_general | solution.py:86
  814.1 25.3 %fusion.158 = f32[768,6144,1]{1,0,2:T(8,128)} fusion(bf16[4,512,768]{1,2,0:T(8,128)(2,1)S(1)} %bitcast.305, bf16[4,512,6144]{2,1,0:T(8,128)(2,1)} %all-gather.11.cloned.1.call-done), kind=kOutput, calls=%fused_computation.188 | convolution fusion | flops 19327352832 | bytes 47185920 | tf_op jit(solution)/shard_map/bse,bsd->ed/dot_general | solution.py:87
  839.4 35.0 %bitcast_add_fusion = f32[768,6144]{1,0:T(8,128)} fusion(f32[768,6144,1]{1,0,2:T(8,128)} %fusion.158, bf16[4,512,768]{1,2,0:T(8,128)(2,1)S(1)} %bitcast.309, bf16[4,512,6144]{2,1,0:T(8,128)(2,1)} %all-gather.13.cloned.1.call-done), kind=kOutput, calls=%fused_computation.20 | convolution fusion | flops 19332071424 | bytes 66060288 | tf_op jit(solution)/shard_map/bse,bsd->ed/dot_general | solution.py:87
  874.4 33.2 %bitcast_add_fusion.1 = f32[6144,768]{1,0:T(8,128)} fusion(f32[6144,768,1]{1,0,2:T(8,128)} %fusion.157, bf16[4,512,6144]{2,1,0:T(8,128)(2,1)} %all-gather.9.cloned.1.call-done, bf16[4,512,768]{1,2,0:T(8,128)(2,1)} %bitcast.307), kind=kOutput, calls=%fused_computation.21 | convolution fusion | flops 19332071424 | bytes 66060288 | tf_op jit(solution)/shard_map/bsd,bse->de/dot_general | solution.py:86
  910.7 13.0 %all_gather.35 = bf16[2,512,256]{2,1,0:T(8,128)(2,1)S(1)} all-gather(bf16[2,64,256]{2,1,0:T(8,128)(2,1)S(1)} %copy.146), channel_id=1, replica_groups=mesh['dp'=2,'tp'=8] {'tp'}, dimensions={1}, use_global_device_ids=true | all-gather | bytes 589824 | tf_op jit(solution)/shard_map/all_gather | solution.py:53
  923.7 12.3 %all_gather.34 = bf16[2,512,256]{2,1,0:T(8,128)(2,1)S(1)} all-gather(bf16[2,64,256]{2,1,0:T(8,128)(2,1)S(1)} %copy.147), channel_id=1, replica_groups=mesh['dp'=2,'tp'=8] {'tp'}, dimensions={1}, use_global_device_ids=true | all-gather | bytes 589824 | tf_op jit(solution)/shard_map/all_gather | solution.py:53
  936.1 11.8 all_gather.37
  947.8 12.3 %all_gather.36 = bf16[2,512,256]{2,1,0:T(8,128)(2,1)S(1)} all-gather(bf16[2,64,256]{2,1,0:T(8,128)(2,1)S(1)} %copy.149), channel_id=1, replica_groups=mesh['dp'=2,'tp'=8] {'tp'}, dimensions={1}, use_global_device_ids=true | all-gather | bytes 589824 | tf_op jit(solution)/shard_map/all_gather | solution.py:53
  961.3 6.4 fusion.79
  967.7 13.2 %convolution_bitcast_fusion.1 = f32[6144,256]{1,0:T(8,128)S(1)} fusion(bf16[4,512,6144]{2,1,0:T(8,128)(2,1)} %all-gather.7.cloned.1.call-done, bf16[2,512,256]{2,1,0:T(8,128)(2,1)S(1)} %all_gather.35, bf16[2,512,256]{2,1,0:T(8,128)(2,1)S(1)} %all_gather.34), kind=kOutput, calls=%fused_computation.61 | convolution fusion | flops 6442975232 | bytes 32505856 | tf_op jit(solution)/shard_map/bsd,bsc->dc/dot_general | solution.py:96
  980.9 14.4 %fusion.36 = f32[6144,256]{1,0:T(8,128)} fusion(f32[6144,256]{1,0:T(8,128)S(1)} %convolution_bitcast_fusion.1, bf16[4,512,6144]{2,1,0:T(8,128)(2,1)} %all-gather.9.cloned.1.call-done, bf16[2,512,256]{2,1,0:T(8,128)(2,1)S(1)} %all_gather.37, bf16[2,512,256]{2,1,0:T(8,128)(2,1)S(1)} %all_gather.36), kind=kOutput, calls=%fused_computation.60 | convolution fusion | flops 6444548096 | bytes 38797312 | tf_op jit(solution)/shard_map/bsd,bsc->dc/dot_general | solution.py:96
  995.3 6.3 fusion.65
  1003.7 7.2 fusion.64
  1011.0 7.5 fusion.56
  1018.5 9.9 fusion.55
  1033.0 10.7 all-gather.1
  1045.7 116.9 %reduce-scatter.5.cloned.1.call-done = bf16[4,64,6144]{2,1,0:T(8,128)(2,1)} async-done(((bf16[4,512,6144]{2,1,0:T(8,128)(2,1)}), bf16[4,64,6144]{2,1,0:T(8,128)(2,1)}) %reduce-scatter.5.cloned.1.call-update) | async-done | bytes 3145744 | tf_op jit(solution)/shard_map/reduce_scatter | solution.py:79
  1162.6 5.9 fusion.68
  (131 shorter events, 47.7 us)
Async XLA Ops:
  7.2 291.3 %copy-start = (bf16[6144,256]{1,0:T(8,128)(2,1)S(1)}, bf16[6144,256]{1,0:T(8,128)(2,1)}, u32[]{:S(2)}) copy-start(bf16[6144,256]{1,0:T(8,128)(2,1)} %param.15) | copy-start | bytes 9437188
  7.2 136.0 %all-gather.7.cloned.1.call-start = ((), (), s32[]{:S(2)}) async-start(), calls=%async_computation.5 | async-start | bytes 28311552 | tf_op jit(solution)/shard_map/all_gather | solution.py:53
  7.2 4.8 copy-start.1
  7.2 6.8 copy-start.8
  7.3 6.7 copy-start.27
  11.2 7.5 copy-start.18
  11.2 7.5 copy-start.20
  14.0 4.7 copy-start.24
  14.0 4.7 copy-start.22
  18.7 248.3 %all-gather.11.cloned.1.call-start = ((), (), s32[]{:S(2)}) async-start(), calls=%async_computation.8 | async-start | bytes 28311552 | tf_op jit(solution)/shard_map/all_gather | solution.py:53
  25.1 118.1 %copy-start.30 = (f32[768]{0:T(1024)S(1)}, f32[768]{0:T(1024)}, u32[]{:S(2)}) copy-start(f32[768]{0:T(1024)} %param.14) | copy-start | bytes 9220
  25.1 404.6 %all-gather.9.cloned.1.call-start = ((), (), s32[]{:S(2)}) async-start(), calls=%async_computation.7 | async-start | bytes 28311552 | tf_op jit(solution)/shard_map/all_gather | solution.py:53
  25.8 488.9 %all-gather.13.cloned.1.call-start = ((), (), s32[]{:S(2)}) async-start(), calls=%async_computation.11 | async-start | bytes 28311552 | tf_op jit(solution)/shard_map/all_gather | solution.py:53
  26.4 968.9 %reduce-scatter.9.cloned.1.call-start = ((), (), s32[]{:S(2)}) async-start(), calls=%async_computation.10 | async-start | bytes 28311552 | tf_op jit(solution)/shard_map/reduce_scatter | solution.py:85
  26.6 290.7 %copy-start.15 = (pred[512,512]{0,1:T(8,128)(4,1)}, pred[512,512]{0,1:T(8,128)(4,1)S(1)}, u32[]{:S(2)}) copy-start(pred[512,512]{0,1:T(8,128)(4,1)S(1)} %iota_compare_fusion) | copy-start | bytes 786436
  293.8 4.7 copy-start.32
  298.5 11.9 %copy-start.5 = (bf16[4,512,768]{1,2,0:T(8,128)(2,1)S(1)}, bf16[4,512,768]{1,2,0:T(8,128)(2,1)}, u32[]{:S(2)}) copy-start(bf16[4,512,768]{1,2,0:T(8,128)(2,1)} %copy.80) | copy-start | bytes 9437188
  310.4 6.8 copy-start.14
  332.6 56.6 %copy-start.38 = (f32[4,6,512]{2,1,0:T(8,128)}, f32[4,6,512]{2,1,0:T(8,128)S(1)}, u32[]{:S(2)}) copy-start(f32[4,6,512]{2,1,0:T(8,128)S(1)} %get-tuple-element.49) | copy-start | bytes 147460
  389.1 621.8 %reduce-scatter.11.cloned.1.call-start = ((), (), s32[]{:S(2)}) async-start(), calls=%async_computation.12 | async-start | bytes 28311552 | tf_op jit(solution)/shard_map/reduce_scatter | solution.py:85
  401.3 28.4 %copy-start.31 = (f32[768]{0:T(1024)S(1)}, f32[768]{0:T(1024)}, u32[]{:S(2)}) copy-start(f32[768]{0:T(1024)} %param.14) | copy-start | bytes 9220
  541.7 5.2 copy-start.33
  546.9 12.6 %copy-start.7 = (bf16[4,512,768]{1,2,0:T(8,128)(2,1)S(1)}, bf16[4,512,768]{1,2,0:T(8,128)(2,1)}, u32[]{:S(2)}) copy-start(bf16[4,512,768]{1,2,0:T(8,128)(2,1)} %copy.92) | copy-start | bytes 9437188
  559.4 6.6 copy-start.13
  559.5 6.6 copy-start.16
  639.3 393.6 %reduce-scatter.7.cloned.1.call-start = ((), (), s32[]{:S(2)}) async-start(), calls=%async_computation.9 | async-start | bytes 28311552 | tf_op jit(solution)/shard_map/reduce_scatter | solution.py:79
  650.4 1.7 copy-start.36
  679.2 7.0 copy-start.39
  679.2 483.4 %reduce-scatter.5.cloned.1.call-start = ((), (), s32[]{:S(2)}) async-start(), calls=%async_computation.6 | async-start | bytes 28311552 | tf_op jit(solution)/shard_map/reduce_scatter | solution.py:79
  679.2 6.9 copy-start.6
  764.8 11.9 %copy-start.10 = (bf16[4,512,128]{1,2,0:T(8,128)(2,1)S(1)}, bf16[4,512,128]{1,2,0:T(8,128)(2,1)}, u32[]{:S(2)}) copy-start(bf16[4,512,128]{1,2,0:T(8,128)(2,1)} %fusion.124) | copy-start | bytes 1572868
  764.8 11.9 %copy-start.11 = (bf16[4,512,128]{1,2,0:T(8,128)(2,1)S(1)}, bf16[4,512,128]{1,2,0:T(8,128)(2,1)}, u32[]{:S(2)}) copy-start(bf16[4,512,128]{1,2,0:T(8,128)(2,1)} %fusion.119) | copy-start | bytes 1572868
  764.8 11.9 %copy-start.12 = (bf16[4,512,128]{1,2,0:T(8,128)(2,1)S(1)}, bf16[4,512,128]{1,2,0:T(8,128)(2,1)}, u32[]{:S(2)}) copy-start(bf16[4,512,128]{1,2,0:T(8,128)(2,1)} %fusion.120) | copy-start | bytes 1572868
  782.7 125.6 %all-to-all-start = ((bf16[8,512,256]{2,0,1:T(8,128)(2,1)}), bf16[8,512,256]{2,0,1:T(8,128)(2,1)}, u32[]{:S(2)}, u32[]{:S(2)}) async-start(bf16[8,512,256]{2,0,1:T(8,128)(2,1)} %copy.96), calls=%async_computation.3 | async-start | bytes 4194304 | tf_op jit(solution)/shard_map/all_to_all | solution.py:91
  787.5 26.6 %copy-start.35 = (bf16[4,128,6,512]{3,1,2,0:T(8,128)(2,1)S(1)}, bf16[4,128,6,512]{3,1,2,0:T(8,128)(2,1)}, u32[]{:S(2)}) copy-start(bf16[4,128,6,512]{3,1,2,0:T(8,128)(2,1)} %copy-done.34) | copy-start | bytes 9437188
  814.1 25.3 %copy-start.37 = (bf16[4,128,6,512]{3,1,2,0:T(8,128)(2,1)S(1)}, bf16[4,128,6,512]{3,1,2,0:T(8,128)(2,1)}, u32[]{:S(2)}) copy-start(bf16[4,128,6,512]{3,1,2,0:T(8,128)(2,1)} %copy-done.36) | copy-start | bytes 9437188
  874.4 33.2 %copy-start.28 = (f32[6,128]{1,0:T(8,128)S(1)}, f32[6,128]{1,0:T(8,128)}, u32[]{:S(2)}) copy-start(f32[6,128]{1,0:T(8,128)} %get-tuple-element.53) | copy-start | bytes 9220
  874.4 33.2 %copy-start.29 = (f32[6,128]{1,0:T(8,128)S(1)}, f32[6,128]{1,0:T(8,128)}, u32[]{:S(2)}) copy-start(f32[6,128]{1,0:T(8,128)} %get-tuple-element.55) | copy-start | bytes 9220
  980.9 14.4 %copy-start.9 = (f32[6144]{0:T(1024)S(1)}, f32[6144]{0:T(1024)}, u32[]{:S(2)}) copy-start(f32[6144]{0:T(1024)} %param.11) | copy-start | bytes 73732
  980.9 14.4 %copy-start.21 = (f32[4,64]{1,0:T(4,128)S(1)}, f32[4,64]{1,0:T(4,128)}, u32[]{:S(2)}) copy-start(f32[4,64]{1,0:T(4,128)} %copy-done.20) | copy-start | bytes 3076
  980.9 14.4 %copy-start.25 = (f32[4,64]{1,0:T(4,128)S(1)}, f32[4,64]{1,0:T(4,128)}, u32[]{:S(2)}) copy-start(f32[4,64]{1,0:T(4,128)} %copy-done.24) | copy-start | bytes 3076
  995.3 8.4 copy-start.2
  1003.7 7.2 copy-start.19
  1003.7 7.2 copy-start.23
  1011.0 7.5 copy-start.3
  1018.5 10.0 copy-start.4
  1028.5 4.4 copy-start.17
  1028.5 134.1 %copy-start.26 = (f32[6144]{0:T(1024)S(1)}, f32[6144]{0:T(1024)}, u32[]{:S(2)}) copy-start(f32[6144]{0:T(1024)} %param.18) | copy-start | bytes 73732
  (1 other events, 1.7 us)
Sparse Core Ops, SparseCore 0:
  18.9 124.2 all-gather.6
  145.6 121.4 all-gather.10
  269.5 121.4 all-gather.8
  393.3 121.4 all-gather.12
  518.2 150.6 reduce-scatter.8
  672.3 173.1 reduce-scatter.10
  849.1 159.1 reduce-scatter.6
  1011.8 150.7 reduce-scatter.4
